TPU v7x, 32 devices: a whole 2x2x4 slice. The times are simulated.
32 devices in a mesh: dom: 8 (over z, y), edge: 4 (over x, core).
Axes of the slice: x: 2, y: 2, z: 4, core: 2. Of those that a mesh axis runs over, the one named last changes fastest.
Arguments:
- fine_nodes: bfloat16 [65536, 128], P('dom'), may hold values from -6 to 6
- fine_edges: bfloat16 [131072, 128], P(('dom', 'edge')), may hold values from -6 to 6
- fine_senders: int32 [131072], P(('dom', 'edge')), may hold values from 0 to 8703, as said below
- fine_receivers: int32 [131072], P(('dom', 'edge')), may hold values from 0 to 8191
- fine_halo: int32 [8, 8, 64], P('dom'), may hold values from 0 to 8191
- coarse_edges: bfloat16 [32768, 128], P(('dom', 'edge')), may hold values from -6 to 6
- coarse_senders: int32 [32768], P(('dom', 'edge')), may hold values from 0 to 2303, as said below
- coarse_receivers: int32 [32768], P(('dom', 'edge')), may hold values from 0 to 2047
- coarse_halo: int32 [8, 8, 32], P('dom'), may hold values from 0 to 2047
- pool_send: int32 [8, 8, 1536], P('dom'), may hold values from 0 to 8191, as said below
- pool_dest: int32 [8, 8, 1536], P('dom'), may hold values from 0 to 2048, as said below
- unpool_slot: int32 [65536], P('dom'), may hold values from 0 to 12287, as said below
- edge_in_weight: bfloat16 [2, 384, 128], replicated, may hold values from -0.3125 to 0.3125
- edge_out_weight: bfloat16 [2, 128, 128], replicated, may hold values from -0.5 to 0.5
- node_in_weight: bfloat16 [2, 256, 128], replicated, may hold values from -0.375 to 0.375
- node_out_weight: bfloat16 [2, 128, 128], replicated, may hold values from -0.5 to 0.5
- edge_gain: float32 [2, 128], replicated, may hold values from 0.5 to 1.5
- node_gain: float32 [2, 128], replicated, may hold values from 0.5 to 1.5
Outputs:
- fine_out: bfloat16 [65536, 128], P('dom')
- coarse_out: bfloat16 [16384, 128], P('dom')
Inputs may be any that keep to these rules, and one draw needn't show every extreme that they name: `fine_senders`: an entry below 8192 is a row of the edge's own partition; an entry 8192 + d * 64 + s names slot s of fine_halo[d, p] for the edge's partition p. `coarse_senders`: an entry below 2048 is a row of the edge's own coarse partition; an entry 2048 + d * 32 + s names slot s of coarse_halo[d, p]. pool_send[d, p, s] is a row of partition d. For each pair (d, p) the slots that carry data come first and number at most 1536; in every draw some p receives 1536 from every d. Every row of partition d is carried exactly once over all p and s; empty slots hold 0. pool_dest[p, d, s] is 2048 exactly where slot s of pool_send[d, p] is empty, else a row of coarse partition p. `unpool_slot`: row r of partition d holds p * 1536 + s for the one carrying slot with pool_send[d, p, s] = r.
All inputs are finite; a program needn't handle non-finite values.
Results may differ from a plain program's by a relative error of at most 0.0068.
Values may be sent and summed in bfloat16 or wider, within the bound.
No kernel may reach another device: no remote copies, remote signals or barrier semaphores. Data moves between devices by JAX's collectives and lax.ppermute only.
A program may use at most 64 MiB of HBM per device.

v0:
```python
import jax
import jax.numpy as jnp
from jax import lax
from jax.sharding import PartitionSpec as P

COARSE = 2048


def layer_norm(values, gain):
    center = values - jnp.mean(values, axis=-1, keepdims=True)
    spread = jnp.mean(center * center, axis=-1, keepdims=True)
    return center * lax.rsqrt(spread + 1e-05) * gain


def node_update(rows, summed, w_first, w_second, gain):
    inputs = jnp.concatenate([rows, summed.astype(jnp.bfloat16)], axis=1)
    hidden = jax.nn.silu(jnp.dot(inputs, w_first, preferred_element_type=jnp.float32)).astype(
        jnp.bfloat16
    )
    result = layer_norm(jnp.dot(hidden, w_second, preferred_element_type=jnp.float32), gain)
    return (rows.astype(jnp.float32) + result).astype(jnp.bfloat16)


def graph_layer(nodes, edges, senders, receivers, border, level, weights):
    edge_in_weight, edge_out_weight, node_in_weight, node_out_weight, edge_gain, node_gain = weights
    width = nodes.shape[-1]
    outgoing = nodes[border[0]]
    ghosts = lax.all_to_all(outgoing, "dom", split_axis=0, concat_axis=0, tiled=True)
    table = jnp.concatenate([nodes, ghosts.reshape(-1, width)], axis=0)
    inputs = jnp.concatenate([table[senders], nodes[receivers], edges], axis=1)
    hidden = jax.nn.silu(
        jnp.dot(inputs, edge_in_weight[level], preferred_element_type=jnp.float32)
    ).astype(jnp.bfloat16)
    message = layer_norm(
        jnp.dot(hidden, edge_out_weight[level], preferred_element_type=jnp.float32),
        edge_gain[level],
    )
    partial_sum = jax.ops.segment_sum(message, receivers, num_segments=nodes.shape[0])
    summed = lax.psum(partial_sum, "edge")
    return node_update(
        nodes, summed, node_in_weight[level], node_out_weight[level], node_gain[level]
    )


def pooled_mean(arrived, places, width):
    sums = jax.ops.segment_sum(
        arrived.reshape(-1, width).astype(jnp.float32), places, num_segments=COARSE + 1
    )[:COARSE]
    counts = jax.ops.segment_sum(jnp.ones_like(places), places, num_segments=COARSE + 1)[:COARSE]
    return (sums / jnp.maximum(counts, 1).astype(jnp.float32)[:, None]).astype(jnp.bfloat16)


def shards(
    fine_nodes,
    fine_edges,
    fine_senders,
    fine_receivers,
    fine_halo,
    coarse_edges,
    coarse_senders,
    coarse_receivers,
    coarse_halo,
    pool_send,
    pool_dest,
    unpool_slot,
    edge_in_weight,
    edge_out_weight,
    node_in_weight,
    node_out_weight,
    edge_gain,
    node_gain,
):
    weights = (
        edge_in_weight,
        edge_out_weight,
        node_in_weight,
        node_out_weight,
        edge_gain,
        node_gain,
    )
    width = fine_nodes.shape[-1]
    fine_mid = graph_layer(
        fine_nodes, fine_edges, fine_senders, fine_receivers, fine_halo, 0, weights
    )
    places = pool_dest[0].reshape(-1)
    arrived = lax.all_to_all(fine_mid[pool_send[0]], "dom", split_axis=0, concat_axis=0, tiled=True)
    coarse_in = pooled_mean(arrived, places, width)
    coarse_out = graph_layer(
        coarse_in, coarse_edges, coarse_senders, coarse_receivers, coarse_halo, 1, weights
    )
    padded = jnp.concatenate([coarse_out, jnp.zeros((1, width), jnp.bfloat16)], axis=0)
    back = lax.all_to_all(padded[pool_dest[0]], "dom", split_axis=0, concat_axis=0, tiled=True)
    parents = back.reshape(-1, width)[unpool_slot]
    fine_out = (fine_mid.astype(jnp.float32) + parents.astype(jnp.float32)).astype(jnp.bfloat16)
    return (fine_out, coarse_out)


def solution(mesh):
    placed = (
        P("dom", None),
        P(("dom", "edge"), None),
        P(("dom", "edge")),
        P(("dom", "edge")),
        P("dom", None, None),
        P(("dom", "edge"), None),
        P(("dom", "edge")),
        P(("dom", "edge")),
        P("dom", None, None),
        P("dom", None, None),
        P("dom", None, None),
        P("dom"),
        P(),
        P(),
        P(),
        P(),
        P(),
        P(),
    )
    return jax.shard_map(
        shards,
        mesh=mesh,
        in_specs=placed,
        out_specs=(P("dom", None), P("dom", None)),
        check_vma=False,
    )
```

profile of v0, /device:TPU:0, one launch (start us, length us, event | category | flops | bytes accessed | tf_op | source)
XLA Modules:
  0.0 604.5 jit_solution(17450261135767377777)
XLA Ops:
  0.6 0.7 compare_select_fusion.8
  1.4 3.5 gather_fusion
  4.9 7.3 %all-to-all-start = ((bf16[8,64,128]{2,1,0:T(8,128)(2,1)}), bf16[8,64,128]{2,1,0:T(8,128)(2,1)S(1)}, u32[]{:S(2)}, u32[]{:S(2)}) async-start(bf16[8,64,128]{2,1,0:T(8,128)(2,1)} %bitcast.1), calls=%async_computation | async-start | bytes 262144 | tf_op jit(solution)/shard_map/all_to_all | solution.py:28
  12.2 0.7 fusion.77
  13.0 0.8 slice_bitcast_fusion.1
  13.7 1.0 compare_select_fusion.1
  14.7 0.8 slice_bitcast_fusion
  15.5 4.1 copy.24
  19.5 12.1 %gather_fusion.2 = bf16[4096,128]{1,0:T(8,128)(2,1)S(1)} fusion(bf16[8192,128]{1,0:T(8,128)(2,1)S(1)} %copy-done, s32[4096]{0:T(1024)S(1)} %fusion.77), kind=kCustom, calls=%fused_computation.2 | custom fusion | bytes 2113536 | tf_op jit(solution)/shard_map/gather | solution.py:30
  31.7 5.6 pad_maximum_fusion
  37.3 16.2 %gather_fusion.1 = bf16[4096,128]{1,0:T(8,128)(2,1)} fusion(bf16[8704,128]{1,0:T(8,128)(2,1)} %pad_maximum_fusion, s32[4096]{0:T(1024)S(1)} %fusion.76), kind=kCustom, calls=%fused_computation.1 | custom fusion | bytes 2113536 | tf_op jit(solution)/shard_map/gather | solution.py:30
  53.5 4.3 fusion.95
  57.8 2.0 multiply_reduce_fusion.1
  59.8 0.2 copy-done.4
  60.0 1.7 multiply_multiply_fusion
  61.7 2.9 copy.25
  64.6 24.8 %scatter_custom_fusion = f32[8192,128]{1,0:T(8,128)} fusion(s32[4096]{0:T(1024)} %param.21, f32[4096,128]{1,0:T(8,128)} %copy.25, f32[]{:T(128)} %constant.13.clone.1), kind=kCustom, calls=%fused_computation.33 | custom fusion | flops 524288 | bytes 4194816 | tf_op jit(solution)/shard_map/scatter-add | solution.py:38
  89.4 77.1 %all-reduce.3 = bf16[8192,128]{1,0:T(8,128)(2,1)} all-reduce(f32[8192,128]{1,0:T(8,128)} %scatter_custom_fusion), channel_id=1, replica_groups=mesh['dom'=8,'edge'=4] {'edge'}, use_global_device_ids=true, to_apply=%region_3.4 | all-reduce | flops 1048576 | bytes 6291456 | tf_op jit(solution)/shard_map/psum | solution.py:39
  166.5 5.8 fusion.100
  172.3 2.8 multiply_reduce_fusion
  175.1 0.6 copy-done.2
  175.7 3.8 add_convert_fusion.1
  179.5 3.2 copy.26
  182.7 43.3 %gather_fusion.3 = bf16[12288,128]{1,0:T(8,128)(2,1)} fusion(bf16[8192,128]{1,0:T(8,128)(2,1)S(1)} %copy.26, s32[12288]{0:T(1024)S(1)} %broadcast_clamp_fusion.1), kind=kCustom, calls=%fused_computation.3 | custom fusion | bytes 6340608 | tf_op jit(solution)/shard_map/gather | solution.py:86
  226.0 5.5 all-to-all-start.1
  231.7 75.2 %scatter_custom_fusion.2 = s32[2049]{0:T(1024)S(1)} fusion(s32[12288]{0:T(1024)S(1)} %reshape.263, s32[12288]{0:T(1024)S(1)} %broadcast.163, s32[]{:T(128)} %constant.14.clone.1), kind=kCustom, calls=%fused_computation.101 | custom fusion | flops 12288 | bytes 8200 | tf_op jit(solution)/shard_map/scatter-add | solution.py:49
  307.1 76.8 %scatter_custom_fusion.1 = f32[2049,128]{1,0:T(8,128)} fusion(s32[12288]{0:T(1024)S(1)} %reshape.263, bf16[12288,128]{1,0:T(8,128)(2,1)S(1)} %bitcast.78, f32[]{:T(128)} %constant.13.clone.1), kind=kCustom, calls=%fused_computation.13 | custom fusion | flops 3145728 | bytes 4194820 | tf_op jit(solution)/shard_map/scatter-add | solution.py:46
  383.8 1.6 fusion.24
  385.4 1.5 gather_fusion.4
  386.8 11.6 %all-to-all-start.2 = ((bf16[8,32,128]{2,1,0:T(8,128)(2,1)}), bf16[8,32,128]{2,1,0:T(8,128)(2,1)S(1)}, u32[]{:S(2)}, u32[]{:S(2)}) async-start(bf16[8,32,128]{2,1,0:T(8,128)(2,1)} %bitcast.13), calls=%async_computation.2 | async-start | bytes 131072 | tf_op jit(solution)/shard_map/all_to_all | solution.py:28
  398.5 3.2 gather_fusion.6
  401.8 3.6 all-to-all-done.2
  405.4 3.2 gather_fusion.5
  408.7 0.6 fusion.105
  409.5 0.2 copy.27
  409.7 6.3 %scatter_custom_fusion.3 = f32[2048,128]{1,0:T(8,128)S(1)} fusion(s32[1024]{0:T(1024)S(1)} %copy-done.11, f32[1024,128]{1,0:T(8,128)S(1)} %copy.27, f32[]{:T(128)} %constant.13.clone.1), kind=kCustom, calls=%fused_computation.61 | custom fusion | flops 131072 | bytes 1048580 | tf_op jit(solution)/shard_map/scatter-add | solution.py:38
  416.0 25.8 %all-reduce.4 = bf16[2048,128]{1,0:T(8,128)(2,1)S(1)} all-reduce(f32[2048,128]{1,0:T(8,128)S(1)} %scatter_custom_fusion.3), channel_id=1, replica_groups=mesh['dom'=8,'edge'=4] {'edge'}, use_global_device_ids=true, to_apply=%region_11.12 | all-reduce | flops 262144 | bytes 1572864 | tf_op jit(solution)/shard_map/psum | solution.py:39
  441.8 0.9 fusion.110
  442.7 0.6 multiply_reduce_fusion.2
  443.3 1.0 add_convert_fusion.2
  444.3 0.8 copy-done.5
  445.2 43.3 %gather_fusion.7 = bf16[12288,128]{1,0:T(8,128)(2,1)} fusion(bf16[2049,128]{1,0:T(8,128)(2,1)S(1)} %concatenate.27, s32[12288]{0:T(1024)S(1)} %broadcast_clamp_fusion), kind=kCustom, calls=%fused_computation.7 | custom fusion | bytes 6340608 | tf_op jit(solution)/shard_map/gather | solution.py:92
  488.5 3.8 all-to-all-start.3
  492.3 71.3 %all-to-all-done.3 = bf16[8,1536,128]{2,1,0:T(8,128)(2,1)S(1)} async-done(((bf16[8,1536,128]{2,1,0:T(8,128)(2,1)}), bf16[8,1536,128]{2,1,0:T(8,128)(2,1)S(1)}, u32[]{:S(2)}, u32[]{:S(2)}) %all-to-all-start.3) | async-done | bytes 3145760 | tf_op jit(solution)/shard_map/all_to_all | solution.py:92
  563.6 29.2 %gather_fusion.8 = bf16[8192,128]{1,0:T(8,128)(2,1)} fusion(bf16[12288,128]{1,0:T(8,128)(2,1)S(1)} %bitcast.77, s32[8192]{0:T(1024)S(1)} %fusion.67), kind=kCustom, calls=%fused_computation.8 | custom fusion | bytes 4227072 | tf_op jit(solution)/shard_map/gather | solution.py:93
  592.8 4.2 copy.28
  597.1 3.4 add_convert_fusion
  600.5 4.1 copy.29
  (66 shorter events, 0.6 us)
Async XLA Ops:
  4.9 26.8 %all-to-all-start = ((bf16[8,64,128]{2,1,0:T(8,128)(2,1)}), bf16[8,64,128]{2,1,0:T(8,128)(2,1)S(1)}, u32[]{:S(2)}, u32[]{:S(2)}) async-start(bf16[8,64,128]{2,1,0:T(8,128)(2,1)} %bitcast.1), calls=%async_computation | async-start | bytes 262144 | tf_op jit(solution)/shard_map/all_to_all | solution.py:28
  13.7 5.8 copy-start
  19.5 12.1 %copy-start.8 = (s32[4096]{0:T(1024)S(1)}, s32[4096]{0:T(1024)}, u32[]{:S(2)}) copy-start(s32[4096]{0:T(1024)} %param.20) | copy-start | bytes 49156
  37.3 16.2 %copy-start.15 = (bf16[2,128,128]{2,1,0:T(8,128)(2,1)S(1)}, bf16[2,128,128]{2,1,0:T(8,128)(2,1)}, u32[]{:S(2)}) copy-start(bf16[2,128,128]{2,1,0:T(8,128)(2,1)} %param.31) | copy-start | bytes 196612
  57.8 2.2 copy-start.4
  89.4 77.1 %copy-start.14 = (bf16[2,256,128]{2,1,0:T(8,128)(2,1)S(1)}, bf16[2,256,128]{2,1,0:T(8,128)(2,1)}, u32[]{:S(2)}) copy-start(bf16[2,256,128]{2,1,0:T(8,128)(2,1)} %param.32) | copy-start | bytes 393220
  89.4 77.1 %copy-start.17 = (bf16[2,128,128]{2,1,0:T(8,128)(2,1)S(1)}, bf16[2,128,128]{2,1,0:T(8,128)(2,1)}, u32[]{:S(2)}) copy-start(bf16[2,128,128]{2,1,0:T(8,128)(2,1)} %param.33) | copy-start | bytes 196612
  172.3 3.4 copy-start.2
  226.0 5.5 copy-start.6
  226.0 5.5 copy-start.9
  226.0 81.0 %copy-start.10 = (s32[1024]{0:T(1024)S(1)}, s32[1024]{0:T(1024)}, u32[]{:S(2)}) copy-start(s32[1024]{0:T(1024)} %param.24) | copy-start | bytes 12292
  226.0 81.0 %all-to-all-start.1 = ((bf16[8,1536,128]{2,1,0:T(8,128)(2,1)}), bf16[8,1536,128]{2,1,0:T(8,128)(2,1)S(1)}, u32[]{:S(2)}, u32[]{:S(2)}) async-start(bf16[8,1536,128]{2,1,0:T(8,128)(2,1)} %bitcast.79), calls=%async_computation.1 | async-start | bytes 6291456 | tf_op jit(solution)/shard_map/all_to_all | solution.py:86
  307.0 91.4 %copy-start.11 = (s32[1024]{0:T(1024)S(1)}, s32[1024]{0:T(1024)}, u32[]{:S(2)}) copy-start(s32[1024]{0:T(1024)} %param.25) | copy-start | bytes 12292
  386.8 18.5 %all-to-all-start.2 = ((bf16[8,32,128]{2,1,0:T(8,128)(2,1)}), bf16[8,32,128]{2,1,0:T(8,128)(2,1)S(1)}, u32[]{:S(2)}, u32[]{:S(2)}) async-start(bf16[8,32,128]{2,1,0:T(8,128)(2,1)} %bitcast.13), calls=%async_computation.2 | async-start | bytes 131072 | tf_op jit(solution)/shard_map/all_to_all | solution.py:28
  401.7 6.9 %copy-start.12 = (bf16[1024,128]{1,0:T(8,128)(2,1)S(1)}, bf16[1024,128]{1,0:T(8,128)(2,1)}, u32[]{:S(2)}) copy-start(bf16[1024,128]{1,0:T(8,128)(2,1)} %param.23) | copy-start | bytes 786436
  401.7 6.9 %copy-start.13 = (bf16[2,384,128]{2,1,0:T(8,128)(2,1)S(1)}, bf16[2,384,128]{2,1,0:T(8,128)(2,1)}, u32[]{:S(2)}) copy-start(bf16[2,384,128]{2,1,0:T(8,128)(2,1)} %param.30) | copy-start | bytes 589828
  401.7 6.9 %copy-start.16 = (bf16[2,128,128]{2,1,0:T(8,128)(2,1)S(1)}, bf16[2,128,128]{2,1,0:T(8,128)(2,1)}, u32[]{:S(2)}) copy-start(bf16[2,128,128]{2,1,0:T(8,128)(2,1)} %param.31) | copy-start | bytes 196612
  409.5 32.3 %copy-start.18 = (bf16[2,128,128]{2,1,0:T(8,128)(2,1)S(1)}, bf16[2,128,128]{2,1,0:T(8,128)(2,1)}, u32[]{:S(2)}) copy-start(bf16[2,128,128]{2,1,0:T(8,128)(2,1)} %param.33) | copy-start | bytes 196612
  441.8 1.5 copy-start.3
  444.3 0.8 copy-start.5
  488.5 3.8 copy-start.7
  488.5 75.1 %all-to-all-start.3 = ((bf16[8,1536,128]{2,1,0:T(8,128)(2,1)}), bf16[8,1536,128]{2,1,0:T(8,128)(2,1)S(1)}, u32[]{:S(2)}, u32[]{:S(2)}) async-start(bf16[8,1536,128]{2,1,0:T(8,128)(2,1)} %bitcast.80), calls=%async_computation.3 | async-start | bytes 6291456 | tf_op jit(solution)/shard_map/all_to_all | solution.py:92
  592.8 4.2 copy-start.1
where the time goes:
time: 606 us; the launch traced here: 605 us
  other arithmetic  208 us (34%)
  local copies, waits for them, and re-layouts  178 us (29%)
  blocking collectives  103 us (17%)
  waiting for transfers between devices  74.9 us (12%)
  starting transfers between devices  28.2 us (5%)
  matrix products  11.6 us (2%)
    psum x2, blocking collectives, graph_layer(): summed = lax.psum(partial_sum, 'edge')  103 us
    scatter-add x1, other arithmetic, pooled_mean(): jax.ops.segment_sum(arrived.reshape(-1, width).astype(jnp.float32), place...  76.8 us
    scatter-add x1, other arithmetic, pooled_mean(): jax.ops.segment_sum(jnp.ones_like(places), places, num_segments=COARSE + 1)  75.2 us
    all_to_all x1, waiting for transfers between devices, shards(): lax.all_to_all(padded[pool_dest[0]], 'dom', split_axis=0, concat_axis=0,...  71.3 us
    gather x1, local copies, waits for them, and re-layouts, shards(): padded[pool_dest[0]]  43.3 us
    gather x1, local copies, waits for them, and re-layouts, shards(): fine_mid[pool_send[0]]  43.3 us
    gather x4, local copies, waits for them, and re-layouts, graph_layer(): inputs = jnp.concatenate([table[senders], nodes[receivers], edges], axis=1)  34.7 us
    gather x2, local copies, waits for them, and re-layouts, shards(): parents = back.reshape(-1, width)[unpool_slot]  33.5 us
  transfers between devices with their start and end apart: 4, of which 2 were waited for; matrix products, arithmetic and copies ran while one was open for 16% of the time, Pallas kernels for 0%

commit v1 on v0

--- a/solution.py
+++ b/solution.py
@@ -36,7 +36,9 @@
         edge_gain[level],
     )
     partial_sum = jax.ops.segment_sum(message, receivers, num_segments=nodes.shape[0])
-    summed = lax.psum(partial_sum, "edge")
+    summed = partial_sum
+    for hop in (1, 2):
+        summed = summed + lax.ppermute(summed, "edge", [(dev, dev ^ hop) for dev in range(4)])
     return node_update(
         nodes, summed, node_in_weight[level], node_out_weight[level], node_gain[level]
     )

time: 606 us -> 637 us (1.051)
  waiting for transfers between devices: 74.9 us -> 196 us
  blocking collectives: 103 us -> 0 us
  other arithmetic: 208 us -> 217 us
    ppermute x0 -> x4, waiting for transfers between devices: none -> 122 us  [graph_layer(): lax.ppermute(summed, 'edge', [(dev, dev ^ hop) for dev in range(4)])]
    psum x2 -> x0, blocking collectives: 103 us -> none  [graph_layer(): summed = lax.psum(partial_sum, 'edge')]
  transfers between devices with their start and end apart: 4 -> 8, of which waited for: 2 -> 6; matrix products, arithmetic and copies ran while one was open for 16% -> 15% of each run, Pallas kernels for 0% -> 0%
where the time goes in v1:
time: 637 us; the launch traced here: 636 us
  other arithmetic  217 us (34%)
  waiting for transfers between devices  196 us (31%)
  local copies, waits for them, and re-layouts  177 us (28%)
  starting transfers between devices  32 us (5%)
  matrix products  11.5 us (2%)
    ppermute x4, waiting for transfers between devices, graph_layer(): lax.ppermute(summed, 'edge', [(dev, dev ^ hop) for dev in range(4)])  122 us
    scatter-add x1, other arithmetic, pooled_mean(): jax.ops.segment_sum(arrived.reshape(-1, width).astype(jnp.float32), place...  76.7 us
    scatter-add x1, other arithmetic, pooled_mean(): jax.ops.segment_sum(jnp.ones_like(places), places, num_segments=COARSE + 1)  75.2 us
    all_to_all x1, waiting for transfers between devices, shards(): lax.all_to_all(padded[pool_dest[0]], 'dom', split_axis=0, concat_axis=0,...  70.3 us
    gather x1, local copies, waits for them, and re-layouts, shards(): fine_mid[pool_send[0]]  43.6 us
    gather x1, local copies, waits for them, and re-layouts, shards(): padded[pool_dest[0]]  43.6 us
    gather x4, local copies, waits for them, and re-layouts, graph_layer(): inputs = jnp.concatenate([table[senders], nodes[receivers], edges], axis=1)  35.7 us
    gather x2, local copies, waits for them, and re-layouts, shards(): parents = back.reshape(-1, width)[unpool_slot]  33.6 us
  transfers between devices with their start and end apart: 8, of which 6 were waited for; matrix products, arithmetic and copies ran while one was open for 15% of the time, Pallas kernels for 0%

profile of v1, /device:TPU:0, one launch (start us, length us, event | category | flops | bytes accessed | tf_op | source)
XLA Modules:
  0.0 635.6 jit_solution(4483356768285883152)
XLA Ops:
  0.6 0.7 compare_select_fusion.8
  1.4 3.5 gather_fusion
  4.9 7.3 %all-to-all-start = ((bf16[8,64,128]{2,1,0:T(8,128)(2,1)}), bf16[8,64,128]{2,1,0:T(8,128)(2,1)S(1)}, u32[]{:S(2)}, u32[]{:S(2)}) async-start(bf16[8,64,128]{2,1,0:T(8,128)(2,1)} %bitcast.1), calls=%async_computation | async-start | bytes 262144 | tf_op jit(solution)/shard_map/all_to_all | solution.py:28
  12.2 0.7 fusion.77
  13.0 0.8 slice_bitcast_fusion.1
  13.7 13.0 %gather_fusion.2 = bf16[4096,128]{1,0:T(8,128)(2,1)S(1)} fusion(bf16[8192,128]{1,0:T(8,128)(2,1)} %param.18, s32[4096]{0:T(1024)S(1)} %fusion.77), kind=kCustom, calls=%fused_computation.2 | custom fusion | bytes 2113536 | tf_op jit(solution)/shard_map/gather | solution.py:30
  26.8 5.5 pad_maximum_fusion
  32.4 16.3 %gather_fusion.1 = bf16[4096,128]{1,0:T(8,128)(2,1)} fusion(bf16[8704,128]{1,0:T(8,128)(2,1)} %pad_maximum_fusion, s32[4096]{0:T(1024)S(1)} %fusion.76), kind=kCustom, calls=%fused_computation.1 | custom fusion | bytes 2113536 | tf_op jit(solution)/shard_map/gather | solution.py:30
  48.7 4.3 fusion.95
  52.9 2.0 multiply_reduce_fusion.1
  55.2 1.6 multiply_multiply_fusion
  56.8 2.9 copy.25
  59.7 24.8 %scatter_custom_fusion = f32[8192,128]{1,0:T(8,128)} fusion(s32[4096]{0:T(1024)} %param.21, f32[4096,128]{1,0:T(8,128)} %copy.25, f32[]{:T(128)} %constant.13.clone.1), kind=kCustom, calls=%fused_computation.34 | custom fusion | flops 524288 | bytes 4194816 | tf_op jit(solution)/shard_map/scatter-add | solution.py:38
  84.5 7.4 %collective-permute-done = f32[8192,128]{1,0:T(8,128)S(1)} collective-permute-done((f32[8192,128]{1,0:T(8,128)}, f32[8192,128]{1,0:T(8,128)S(1)}, u32[]{:S(2)}, u32[]{:S(2)}) %collective-permute-start) | collective-permute-done | bytes 4194336 | tf_op jit(solution)/shard_map/ppermute | solution.py:41
  91.9 4.7 add.182
  96.6 1.5 collective-permute-start.1
  98.1 2.9 copy.24
  101.1 88.5 %collective-permute-done.1 = f32[8192,128]{1,0:T(8,128)} collective-permute-done((f32[8192,128]{1,0:T(8,128)}, f32[8192,128]{1,0:T(8,128)}, u32[]{:S(2)}, u32[]{:S(2)}) %collective-permute-start.1) | collective-permute-done | bytes 4194336 | tf_op jit(solution)/shard_map/ppermute | solution.py:41
  189.5 5.2 add_convert_fusion.2
  194.8 5.8 fusion.100
  200.6 2.8 multiply_reduce_fusion
  204.0 3.8 add_convert_fusion.1
  207.8 3.2 copy.26
  211.0 43.6 %gather_fusion.3 = bf16[12288,128]{1,0:T(8,128)(2,1)} fusion(bf16[8192,128]{1,0:T(8,128)(2,1)S(1)} %copy.26, s32[12288]{0:T(1024)S(1)} %broadcast_clamp_fusion.1), kind=kCustom, calls=%fused_computation.3 | custom fusion | bytes 6340608 | tf_op jit(solution)/shard_map/gather | solution.py:88
  254.6 6.1 all-to-all-start.1
  260.9 75.2 %scatter_custom_fusion.2 = s32[2049]{0:T(1024)S(1)} fusion(s32[12288]{0:T(1024)S(1)} %reshape.263, s32[12288]{0:T(1024)S(1)} %broadcast.163, s32[]{:T(128)} %constant.14.clone.1), kind=kCustom, calls=%fused_computation.103 | custom fusion | flops 12288 | bytes 8200 | tf_op jit(solution)/shard_map/scatter-add | solution.py:51
  336.2 76.7 %scatter_custom_fusion.1 = f32[2049,128]{1,0:T(8,128)} fusion(s32[12288]{0:T(1024)S(1)} %reshape.263, bf16[12288,128]{1,0:T(8,128)(2,1)S(1)} %bitcast.78, f32[]{:T(128)} %constant.13.clone.1), kind=kCustom, calls=%fused_computation.13 | custom fusion | flops 3145728 | bytes 4194820 | tf_op jit(solution)/shard_map/scatter-add | solution.py:48
  412.9 1.6 fusion.24
  414.5 1.5 gather_fusion.4
  416.0 11.6 %all-to-all-start.2 = ((bf16[8,32,128]{2,1,0:T(8,128)(2,1)}), bf16[8,32,128]{2,1,0:T(8,128)(2,1)S(1)}, u32[]{:S(2)}, u32[]{:S(2)}) async-start(bf16[8,32,128]{2,1,0:T(8,128)(2,1)} %bitcast.13), calls=%async_computation.2 | async-start | bytes 131072 | tf_op jit(solution)/shard_map/all_to_all | solution.py:28
  427.6 3.2 gather_fusion.6
  430.9 3.6 all-to-all-done.2
  434.6 3.2 gather_fusion.5
  438.8 6.3 scatter_custom_fusion.3
  445.2 2.6 collective-permute-done.2
  448.0 1.6 collective-permute-start.3
  449.6 23.7 %collective-permute-done.3 = f32[2048,128]{1,0:T(8,128)S(1)} collective-permute-done((f32[2048,128]{1,0:T(8,128)S(1)}, f32[2048,128]{1,0:T(8,128)S(1)}, u32[]{:S(2)}, u32[]{:S(2)}) %collective-permute-start.3) | collective-permute-done | bytes 1048608 | tf_op jit(solution)/shard_map/ppermute | solution.py:41
  473.4 0.9 fusion.110
  474.2 0.6 multiply_reduce_fusion.2
  474.9 1.0 add_convert_fusion.3
  475.9 0.8 copy-done.5
  476.7 43.6 %gather_fusion.7 = bf16[12288,128]{1,0:T(8,128)(2,1)} fusion(bf16[2049,128]{1,0:T(8,128)(2,1)S(1)} %concatenate.27, s32[12288]{0:T(1024)S(1)} %broadcast_clamp_fusion), kind=kCustom, calls=%fused_computation.7 | custom fusion | bytes 6340608 | tf_op jit(solution)/shard_map/gather | solution.py:94
  520.3 3.8 all-to-all-start.3
  524.1 70.3 %all-to-all-done.3 = bf16[8,1536,128]{2,1,0:T(8,128)(2,1)S(1)} async-done(((bf16[8,1536,128]{2,1,0:T(8,128)(2,1)}), bf16[8,1536,128]{2,1,0:T(8,128)(2,1)S(1)}, u32[]{:S(2)}, u32[]{:S(2)}) %all-to-all-start.3) | async-done | bytes 3145760 | tf_op jit(solution)/shard_map/all_to_all | solution.py:94
  594.5 29.4 %gather_fusion.8 = bf16[8192,128]{1,0:T(8,128)(2,1)} fusion(bf16[12288,128]{1,0:T(8,128)(2,1)S(1)} %bitcast.77, s32[8192]{0:T(1024)S(1)} %fusion.67), kind=kCustom, calls=%fused_computation.8 | custom fusion | bytes 4227072 | tf_op jit(solution)/shard_map/gather | solution.py:95
  623.9 4.2 copy.28
  628.1 3.4 add_convert_fusion
  631.5 4.1 copy.29
  (82 shorter events, 2.6 us)
Async XLA Ops:
  4.9 21.9 %all-to-all-start = ((bf16[8,64,128]{2,1,0:T(8,128)(2,1)}), bf16[8,64,128]{2,1,0:T(8,128)(2,1)S(1)}, u32[]{:S(2)}, u32[]{:S(2)}) async-start(bf16[8,64,128]{2,1,0:T(8,128)(2,1)} %bitcast.1), calls=%async_computation | async-start | bytes 262144 | tf_op jit(solution)/shard_map/all_to_all | solution.py:28
  13.7 13.0 %copy-start.9 = (s32[4096]{0:T(1024)S(1)}, s32[4096]{0:T(1024)}, u32[]{:S(2)}) copy-start(s32[4096]{0:T(1024)} %param.20) | copy-start | bytes 49156
  13.7 13.1 %copy-start = (bf16[8192,128]{1,0:T(8,128)(2,1)S(1)}, bf16[8192,128]{1,0:T(8,128)(2,1)}, u32[]{:S(2)}) copy-start(bf16[8192,128]{1,0:T(8,128)(2,1)} %param.18) | copy-start | bytes 6291460
  32.4 16.3 %copy-start.15 = (bf16[2,384,128]{2,1,0:T(8,128)(2,1)S(1)}, bf16[2,384,128]{2,1,0:T(8,128)(2,1)}, u32[]{:S(2)}) copy-start(bf16[2,384,128]{2,1,0:T(8,128)(2,1)} %param.30) | copy-start | bytes 589828
  32.4 16.3 %copy-start.18 = (bf16[2,128,128]{2,1,0:T(8,128)(2,1)S(1)}, bf16[2,128,128]{2,1,0:T(8,128)(2,1)}, u32[]{:S(2)}) copy-start(bf16[2,128,128]{2,1,0:T(8,128)(2,1)} %param.31) | copy-start | bytes 196612
  52.9 2.2 copy-start.4
  84.5 7.4 %collective-permute-start = (f32[8192,128]{1,0:T(8,128)}, f32[8192,128]{1,0:T(8,128)S(1)}, u32[]{:S(2)}, u32[]{:S(2)}) collective-permute-start(f32[8192,128]{1,0:T(8,128)} %scatter_custom_fusion), channel_id=1, source_target_pairs={{0,1},{1,0},{2,3},{3,2},{4,5},{5,4},{6,7},{7,6},{8,9},{9,8},{10,11... | collective-permute-start | bytes 12582920 | tf_op jit(solution)/shard_map/ppermute | solution.py:41
  96.6 4.4 copy-start.7
  96.6 4.4 copy-start.13
  96.6 92.9 %collective-permute-start.1 = (f32[8192,128]{1,0:T(8,128)}, f32[8192,128]{1,0:T(8,128)}, u32[]{:S(2)}, u32[]{:S(2)}) collective-permute-start(f32[8192,128]{1,0:T(8,128)} %add.182), channel_id=1, source_target_pairs={{0,2},{1,3},{2,0},{3,1},{4,6},{5,7},{6,4},{7,5},{8,10},{9,11},{10,... | collective-permute-start | bytes 12582920 | tf_op jit(solution)/shard_map/ppermute | solution.py:41
  101.0 93.7 %copy-start.16 = (bf16[2,256,128]{2,1,0:T(8,128)(2,1)S(1)}, bf16[2,256,128]{2,1,0:T(8,128)(2,1)}, u32[]{:S(2)}) copy-start(bf16[2,256,128]{2,1,0:T(8,128)(2,1)} %param.32) | copy-start | bytes 393220
  101.0 93.7 %copy-start.20 = (bf16[2,128,128]{2,1,0:T(8,128)(2,1)S(1)}, bf16[2,128,128]{2,1,0:T(8,128)(2,1)}, u32[]{:S(2)}) copy-start(bf16[2,128,128]{2,1,0:T(8,128)(2,1)} %param.33) | copy-start | bytes 196612
  200.6 3.4 copy-start.2
  254.6 6.2 copy-start.6
  254.6 6.2 copy-start.10
  254.6 81.5 %copy-start.11 = (s32[1024]{0:T(1024)S(1)}, s32[1024]{0:T(1024)}, u32[]{:S(2)}) copy-start(s32[1024]{0:T(1024)} %param.24) | copy-start | bytes 12292
  254.6 81.6 %all-to-all-start.1 = ((bf16[8,1536,128]{2,1,0:T(8,128)(2,1)}), bf16[8,1536,128]{2,1,0:T(8,128)(2,1)S(1)}, u32[]{:S(2)}, u32[]{:S(2)}) async-start(bf16[8,1536,128]{2,1,0:T(8,128)(2,1)} %bitcast.79), calls=%async_computation.1 | async-start | bytes 6291456 | tf_op jit(solution)/shard_map/all_to_all | solution.py:88
  336.2 91.4 %copy-start.12 = (s32[1024]{0:T(1024)S(1)}, s32[1024]{0:T(1024)}, u32[]{:S(2)}) copy-start(s32[1024]{0:T(1024)} %param.25) | copy-start | bytes 12292
  416.0 18.5 %all-to-all-start.2 = ((bf16[8,32,128]{2,1,0:T(8,128)(2,1)}), bf16[8,32,128]{2,1,0:T(8,128)(2,1)S(1)}, u32[]{:S(2)}, u32[]{:S(2)}) async-start(bf16[8,32,128]{2,1,0:T(8,128)(2,1)} %bitcast.13), calls=%async_computation.2 | async-start | bytes 131072 | tf_op jit(solution)/shard_map/all_to_all | solution.py:28
  430.9 6.9 %copy-start.14 = (bf16[1024,128]{1,0:T(8,128)(2,1)S(1)}, bf16[1024,128]{1,0:T(8,128)(2,1)}, u32[]{:S(2)}) copy-start(bf16[1024,128]{1,0:T(8,128)(2,1)} %param.23) | copy-start | bytes 786436
  430.9 6.9 %copy-start.19 = (bf16[2,128,128]{2,1,0:T(8,128)(2,1)S(1)}, bf16[2,128,128]{2,1,0:T(8,128)(2,1)}, u32[]{:S(2)}) copy-start(bf16[2,128,128]{2,1,0:T(8,128)(2,1)} %param.31) | copy-start | bytes 196612
  445.1 2.7 collective-permute-start.2
  447.9 25.4 %copy-start.17 = (bf16[2,256,128]{2,1,0:T(8,128)(2,1)S(1)}, bf16[2,256,128]{2,1,0:T(8,128)(2,1)}, u32[]{:S(2)}) copy-start(bf16[2,256,128]{2,1,0:T(8,128)(2,1)} %param.32) | copy-start | bytes 393220
  448.0 25.4 %copy-start.21 = (bf16[2,128,128]{2,1,0:T(8,128)(2,1)S(1)}, bf16[2,128,128]{2,1,0:T(8,128)(2,1)}, u32[]{:S(2)}) copy-start(bf16[2,128,128]{2,1,0:T(8,128)(2,1)} %param.33) | copy-start | bytes 196612
  448.0 25.3 %collective-permute-start.3 = (f32[2048,128]{1,0:T(8,128)S(1)}, f32[2048,128]{1,0:T(8,128)S(1)}, u32[]{:S(2)}, u32[]{:S(2)}) collective-permute-start(f32[2048,128]{1,0:T(8,128)S(1)} %add.199), channel_id=1, source_target_pairs={{0,2},{1,3},{2,0},{3,1},{4,6},{5,7},{6,4},{7,5},{8,10},{9,11},{10,... | collective-permute-start | bytes 3145736 | tf_op jit(solution)/shard_map/ppermute | solution.py:41
  473.4 1.5 copy-start.3
  475.9 0.8 copy-start.5
  520.3 3.8 copy-start.8
  520.3 74.1 %all-to-all-start.3 = ((bf16[8,1536,128]{2,1,0:T(8,128)(2,1)}), bf16[8,1536,128]{2,1,0:T(8,128)(2,1)S(1)}, u32[]{:S(2)}, u32[]{:S(2)}) async-start(bf16[8,1536,128]{2,1,0:T(8,128)(2,1)} %bitcast.80), calls=%async_computation.3 | async-start | bytes 6291456 | tf_op jit(solution)/shard_map/all_to_all | solution.py:94
  623.9 4.2 copy-start.1
